TPU v7x, 32 devices: a whole 2x2x4 slice. The times are simulated.
32 devices in a mesh: section: 4 (over z), expert: 4 (over y, x), dp: 2 (over core).
Axes of the slice: x: 2, y: 2, z: 4, core: 2. Of those that a mesh axis runs over, the one named last changes fastest.
Arguments:
- stash: bfloat16 [4, 256, 2048], P('section', 'dp', 'expert'), may hold values from -6 to 6
- cotangent: bfloat16 [4, 256, 2048], P('section', 'dp', 'expert'), may hold values from -6 to 6
- backward_expert_routes: int32 [4, 256, 2], P('section', 'dp'), may hold values from 0 to 3, all different within a row; in each aligned block of 128 rows (0 to 127, 128 to 255, ..., all dimensions but the last counted through in order) at most 80 rows name the same one
- backward_job_lengths: int32 [4, 4], P('section'), may hold values from 1 to 128, 256 in all within a row
- layer_norm_gains: float32 [4, 2048], P('section'), may hold values from 0.25 to 1.75
- router: bfloat16 [4, 2048, 4], P('section'), may hold values from -0.125 to 0.125
- expert_gate_weight: bfloat16 [4, 2048, 28672], P('section', None, ('expert', 'dp')), may hold values from -0.125 to 0.125
- expert_up_weight: bfloat16 [4, 2048, 28672], P('section', None, ('expert', 'dp')), may hold values from -0.125 to 0.125
- expert_down_weight: bfloat16 [4, 28672, 2048], P('section', ('expert', 'dp')), may hold values from -0.0625 to 0.0625
- adapter_down_maps: bfloat16 [4, 2048, 64], P('section', 'expert'), may hold values from -0.125 to 0.125
- adapter_up_maps: bfloat16 [4, 64, 2048], P('section', None, 'expert'), may hold values from -1.5 to 1.5
Outputs:
- handed_back: bfloat16 [4, 256, 2048], P('section', 'dp', 'expert')
- grad_lora_down: float32 [4, 2048, 64], P('section', 'expert')
- grad_lora_up: float32 [4, 64, 2048], P('section', None, 'expert')
Inputs may be any that keep to these rules, and one draw needn't show every extreme that they name: `backward_expert_routes`: each row names two different experts. In each aligned block of 128 rows (the tokens of one device) no expert is named more than 80 times. `backward_job_lengths`: each row sums to 256.
All inputs are finite; a program needn't handle non-finite values.
Results may differ from a plain program's by a relative error of at most 0.008.
Values may be sent and summed in bfloat16 or wider, within the bound.
A program may use at most 128 MiB of HBM per device.

v0:
```python
import jax
import jax.numpy as jnp
from jax import lax
from jax.sharding import PartitionSpec as P

MODEL_WIDTH = 2048
EXPERTS = 4
ADAPTER_RANK = 16
CAP = 80
EPS = 1e-05
ADAPTER_SCALE = 0.5
HIGH = lax.Precision.HIGHEST


def from_behind(block, axis, distance):
    devices = range(lax.axis_size(axis))
    route = [((i - distance) % len(devices), i) for i in devices]
    return lax.ppermute(block, axis, route)


def job_columns(job_token_lengths, offset, count):
    ends = jnp.cumsum(job_token_lengths, dtype=jnp.int32)
    position = offset + jnp.arange(count, dtype=jnp.int32)
    owner = jnp.sum((ends[None, :] <= position[:, None]).astype(jnp.int32), axis=1, dtype=jnp.int32)
    column_owner = (
        jnp.arange(job_token_lengths.shape[0] * ADAPTER_RANK, dtype=jnp.int32) // ADAPTER_RANK
    )
    return (owner[:, None] == column_owner[None, :]).astype(jnp.float32)


def prepare(whole_batch, norm_gain_vector, router, token_routes):
    expert_values = whole_batch.astype(jnp.float32)
    scale = lax.rsqrt(jnp.mean(expert_values * expert_values, axis=1, keepdims=True) + EPS)
    normalized_input = (expert_values * scale * norm_gain_vector[None, :]).astype(jnp.bfloat16)
    logits = jnp.dot(normalized_input, router, preferred_element_type=jnp.float32)
    labels = jnp.arange(router.shape[1], dtype=jnp.int32)
    first = (token_routes[:, 0:1] == labels[None, :]).astype(jnp.float32)
    second = (token_routes[:, 1:2] == labels[None, :]).astype(jnp.float32)
    upper = jax.nn.sigmoid(jnp.sum(first * logits, axis=1) - jnp.sum(second * logits, axis=1))
    table = upper[:, None] * first + (1.0 - upper)[:, None] * second
    return (expert_values, scale, normalized_input, first, second, upper, table)


def router_grad(gate_grad, first, second, upper):
    spread = jnp.sum(first * gate_grad, axis=1) - jnp.sum(second * gate_grad, axis=1)
    delta = spread * upper * (1.0 - upper)
    return delta[:, None] * (first - second)


def slot_matrix(member, capacity):
    marks = member.astype(jnp.int32)
    ranked = jnp.cumsum(marks, axis=-1, dtype=jnp.int32) - marks
    slots = jnp.arange(capacity, dtype=jnp.int32)
    hit = (ranked[..., None, :] == slots[:, None]) & (marks[..., None, :] == 1)
    return hit.astype(jnp.float32)


def expert_back(
    rows, adapter_gradient_list, expert_gate_weight, expert_up_weight, expert_down_weight
):
    gate = jnp.dot(rows, expert_gate_weight, preferred_element_type=jnp.float32)
    up = jnp.dot(rows, expert_up_weight, preferred_element_type=jnp.float32)
    sig = jax.nn.sigmoid(gate)
    act = gate * sig
    hidden = (act * up).astype(jnp.bfloat16)
    output = jnp.dot(hidden, expert_down_weight, preferred_element_type=jnp.float32)
    gate_term = jnp.sum(adapter_gradient_list.astype(jnp.float32) * output, axis=1)
    back = jnp.dot(adapter_gradient_list, expert_down_weight.T, preferred_element_type=jnp.float32)
    d_gate = (back * up * sig * (1.0 + gate * (1.0 - sig))).astype(jnp.bfloat16)
    d_up = (back * act).astype(jnp.bfloat16)
    d_rows = jnp.dot(d_gate, expert_gate_weight.T, preferred_element_type=jnp.float32) + jnp.dot(
        d_up, expert_up_weight.T, preferred_element_type=jnp.float32
    )
    return (d_rows, gate_term)


def body(
    stash,
    cotangent,
    backward_expert_routes,
    backward_job_lengths,
    layer_norm_gains,
    router,
    expert_gate_weight,
    expert_up_weight,
    expert_down_weight,
    adapter_down_maps,
    adapter_up_maps,
):
    groups = lax.axis_size("expert")
    shards = lax.axis_size("dp")
    column_block = lax.axis_index("expert")
    token_block = lax.axis_index("dp")
    mine = column_block // (groups // EXPERTS)
    s_cols = stash[0]
    gradient_columns = cotangent[0]
    count, width = s_cols.shape
    s_full, g_full = (
        lax.all_gather(s_cols, "expert", axis=1, tiled=True),
        lax.all_gather(gradient_columns, "expert", axis=1, tiled=True),
    )
    norm_gain_vector = layer_norm_gains[0]
    route_w = router[0]
    wg = expert_gate_weight[0]
    wu = expert_up_weight[0]
    wd = expert_down_weight[0]
    down_map_rows = adapter_down_maps[0]
    backward_columns = adapter_up_maps[0]
    col_start = column_block * width
    gain_cols = lax.dynamic_slice_in_dim(norm_gain_vector, col_start, width, 0)
    route_cols = lax.dynamic_slice_in_dim(route_w, col_start, width, 0)
    offset = token_block * count
    backward_mask = job_columns(backward_job_lengths[0], offset, count)
    b_values, b_scale, b_normed, b_first, b_second, b_upper, b_table = prepare(
        s_full, norm_gain_vector, route_w, backward_expert_routes[0]
    )
    labels = jnp.arange(EXPERTS, dtype=jnp.int32)
    own = (labels == mine).astype(jnp.float32)
    b_member = jnp.sum((b_first + b_second) * own[None, :], axis=1)
    b_gate = jnp.sum(b_table * own[None, :], axis=1)
    b_slots = slot_matrix(b_member, CAP)
    b_normed_cols = lax.dynamic_slice_in_dim(b_normed, col_start, width, 1)
    a_full = lax.all_gather(down_map_rows, "expert", axis=0, tiled=True)
    b_low = jnp.dot(b_normed, a_full, preferred_element_type=jnp.float32)
    grad_low_rank = lax.psum(
        jnp.dot(gradient_columns, backward_columns.T, preferred_element_type=jnp.float32), "expert"
    )
    backward_low_rank = (b_low * backward_mask).astype(jnp.bfloat16)
    grad_low_rank_backward = (ADAPTER_SCALE * grad_low_rank * backward_mask).astype(jnp.bfloat16)
    up_map_gradient = ADAPTER_SCALE * jnp.dot(
        backward_low_rank.T, gradient_columns, preferred_element_type=jnp.float32
    )
    down_map_gradient = jnp.dot(
        b_normed_cols.T, grad_low_rank_backward, preferred_element_type=jnp.float32
    )
    down_map_gradient, up_map_gradient = lax.psum((down_map_gradient, up_map_gradient), "dp")
    normalized_grad_adapter = jnp.dot(
        grad_low_rank_backward, down_map_rows.T, preferred_element_type=jnp.float32
    )
    b_slots_low = b_slots.astype(jnp.bfloat16)
    b_sel = jnp.dot(b_slots_low, b_normed, preferred_element_type=jnp.float32).astype(jnp.bfloat16)
    g_sel = jnp.dot(b_slots_low, g_full, preferred_element_type=jnp.float32).astype(jnp.bfloat16)
    b_rows, g_rows = (
        lax.all_gather(b_sel, "dp", axis=0, tiled=True),
        lax.all_gather(g_sel, "dp", axis=0, tiled=True),
    )
    dn_slots, dgam_slots = expert_back(b_rows, g_rows, wg, wu, wd)
    b_member_all, b_gate_all = (
        lax.all_gather(b_member, "dp", axis=0, tiled=True),
        lax.all_gather(b_gate, "dp", axis=0, tiled=True),
    )
    b_all = slot_matrix(b_member_all.reshape(shards, count), CAP)
    b_terms = jnp.einsum(
        "pct,pcex->eptx", b_all, dn_slots.reshape(shards, CAP, groups, width), precision=HIGH
    )
    b_terms = b_terms * b_gate_all.reshape(shards, count)[None, :, :, None]
    normalized_grad_experts = lax.psum_scatter(
        b_terms.reshape(groups * shards * count, width),
        ("expert", "dp"),
        scatter_dimension=0,
        tiled=True,
    )
    dgam_own = lax.psum_scatter(dgam_slots, "dp", scatter_dimension=0, tiled=True)
    dgam_tokens = jnp.dot(dgam_own, b_slots, precision=HIGH)
    gate_part = dgam_tokens[:, None] * own[None, :]
    expert_base_output = normalized_grad_experts + normalized_grad_adapter
    b_values_cols = lax.dynamic_slice_in_dim(b_values, col_start, width, 1)
    route_cols_t = route_cols.astype(jnp.float32).T
    base_weighted = expert_base_output * gain_cols[None, :]
    stat_part = jnp.sum(base_weighted * b_values_cols, axis=1, keepdims=True)
    gate_grad, stat_part = lax.psum((gate_part, stat_part), "expert")
    d_logit = router_grad(gate_grad, b_first, b_second, b_upper)
    lifted = jnp.dot(
        b_values * norm_gain_vector[None, :], route_w.astype(jnp.float32), precision=HIGH
    )
    stat = stat_part + jnp.sum(d_logit * lifted, axis=1, keepdims=True)
    weighted = base_weighted + jnp.dot(d_logit, route_cols_t, precision=HIGH) * gain_cols[None, :]
    layer_result = (
        gradient_columns.astype(jnp.float32)
        + b_scale * weighted
        - b_values_cols * b_scale * b_scale * b_scale * stat / MODEL_WIDTH
    )
    handed_back = from_behind(layer_result.astype(jnp.bfloat16), "section", -1)
    return (handed_back[None], down_map_gradient[None], up_map_gradient[None])


def solution(mesh):
    return jax.shard_map(
        body,
        mesh=mesh,
        in_specs=(
            P("section", "dp", "expert"),
            P("section", "dp", "expert"),
            P("section", "dp", None),
            P("section", None),
            P("section", None),
            P("section", None, None),
            P("section", None, ("expert", "dp")),
            P("section", None, ("expert", "dp")),
            P("section", ("expert", "dp"), None),
            P("section", "expert", None),
            P("section", None, "expert"),
        ),
        out_specs=(
            P("section", "dp", "expert"),
            P("section", "expert", None),
            P("section", None, "expert"),
        ),
        check_vma=False,
    )
```

profile of v0, /device:TPU:0, one launch (start us, length us, event | category | flops | bytes accessed | tf_op | source)
XLA Modules:
  0.0 168.8 jit_solution(5793704472606777799)
XLA Ops:
  8.1 12.0 %all-gather = bf16[1,128,2048]{2,1,0:T(8,128)(2,1)S(1)} all-gather(bf16[1,128,512]{2,1,0:T(8,128)(2,1)} %param.11), channel_id=2, replica_groups=mesh['section'=4,'expert'=4,'dp'=2] {'expert'}, dimensions={2}, use_global_device_ids=true | all-gather | bytes 655360 | tf_op jit(solution)/shard_map/all_gather | solution.py:99
  23.0 1.8 %all-gather.3 = f32[2,1,128]{2,1,0:T(1,128)S(1)} all-gather(f32[1,1,128]{2,1,0:T(1,128)S(1)} %bitcast.144), channel_id=1, replica_groups=mesh['section'=4,'expert'=4,'dp'=2] {'dp'}, dimensions={0}, use_global_device_ids=true | all-gather | bytes 1536 | tf_op jit(solution)/shard_map/all_gather | solution.py:149
  25.3 9.7 %all-gather.1 = bf16[1,128,2048]{2,1,0:T(8,128)(2,1)S(1)} all-gather(bf16[1,128,512]{2,1,0:T(8,128)(2,1)S(1)} %copy-done.2), channel_id=3, replica_groups=mesh['section'=4,'expert'=4,'dp'=2] {'expert'}, dimensions={2}, use_global_device_ids=true | all-gather | bytes 655360 | tf_op jit(solution)/shard_map/all_gather | solution.py:100
  35.4 2.3 %all_gather.23 = bf16[160,2048]{1,0:T(8,128)(2,1)S(1)} all-gather(bf16[80,2048]{1,0:T(8,128)(2,1)S(1)} %convolution_convert_fusion.1), channel_id=1, replica_groups=mesh['section'=4,'expert'=4,'dp'=2] {'dp'}, dimensions={0}, use_global_device_ids=true | all-gather | bytes 983040 | tf_op jit(solution)/shard_map/all_gather | solution.py:145
  37.7 2.3 %all_gather.24 = bf16[160,2048]{1,0:T(8,128)(2,1)S(1)} all-gather(bf16[80,2048]{1,0:T(8,128)(2,1)S(1)} %convolution_convert_fusion), channel_id=1, replica_groups=mesh['section'=4,'expert'=4,'dp'=2] {'dp'}, dimensions={0}, use_global_device_ids=true | all-gather | bytes 983040 | tf_op jit(solution)/shard_map/all_gather | solution.py:144
  40.0 9.3 %fusion.2 = f32[160,3584]{1,0:T(8,128)} fusion(bf16[160,2048]{1,0:T(8,128)(2,1)S(1)} %all_gather.24, bf16[1,2048,3584]{2,1,0:T(8,128)(2,1)} %param.17), kind=kOutput, calls=%fused_computation.2 | convolution fusion | flops 2348810240 | bytes 17629184 | tf_op jit(solution)/shard_map/dot_general | solution.py:61
  50.1 3.9 %fusion.6 = f32[160,3584]{1,0:T(8,128)} fusion(bf16[160,2048]{1,0:T(8,128)(2,1)S(1)} %all_gather.24, bf16[1,2048,3584]{2,1,0:T(8,128)(2,1)S(1)} %copy-done.1), kind=kOutput, calls=%fused_computation.6 | convolution fusion | flops 2348810240 | bytes 17629184 | tf_op jit(solution)/shard_map/dot_general | solution.py:62
  54.1 11.6 %fusion.10 = f32[160,3584]{1,0:T(8,128)} fusion(bf16[160,2048]{1,0:T(8,128)(2,1)S(1)} %all_gather.23, bf16[1,3584,2048]{2,1,0:T(8,128)(2,1)} %param.19), kind=kOutput, calls=%fused_computation.10 | convolution fusion | flops 2348810240 | bytes 17629184 | tf_op jit(solution)/shard_map/dot_general | solution.py:68
  65.7 12.1 %fusion = f32[160,2048]{1,0:T(8,128)S(1)} fusion(bf16[1,2048,3584]{2,1,0:T(8,128)(2,1)} %param.17, f32[160,3584]{1,0:T(8,128)} %fusion.2, f32[160,3584]{1,0:T(8,128)} %fusion.10, f32[160,3584]{1,0:T(8,128)} %fusion.6), kind=kOutput, calls=%fused_computation | convolution fusion | flops 2354544640 | bytes 22872064 | tf_op jit(solution)/shard_map/dot_general | solution.py:71
  77.8 12.7 %fusion.15 = f32[160,2048]{1,0:T(8,128)} fusion(f32[160,2048]{1,0:T(8,128)S(1)} %fusion, bf16[1,2048,3584]{2,1,0:T(8,128)(2,1)} %param.18, f32[160,3584]{1,0:T(8,128)} %fusion.10, f32[160,3584]{1,0:T(8,128)} %fusion.2), kind=kOutput, calls=%fused_computation.13 | convolution fusion | flops 2352578560 | bytes 21889024 | tf_op jit(solution)/shard_map/dot_general | solution.py:71
  90.5 2.2 %reshape.159 = f32[2,80,4,512]{3,2,1,0:T(4,128)S(1)} reshape(f32[160,2048]{1,0:T(8,128)} %fusion.15) | data formatting | bytes 2621440 | tf_op jit(solution)/shard_map/reshape | solution.py:154
  93.0 1.8 %all-gather.4 = f32[2,1,128]{2,1,0:T(1,128)S(1)} all-gather(f32[1,1,128]{2,1,0:T(1,128)S(1)} %bitcast.143), channel_id=1, replica_groups=mesh['section'=4,'expert'=4,'dp'=2] {'dp'}, dimensions={0}, use_global_device_ids=true | all-gather | bytes 1536 | tf_op jit(solution)/shard_map/all_gather | solution.py:150
  94.8 1.5 multiply_bitcast_fusion
  96.4 1.6 copy.28
  98.4 15.4 %psum.35 = f32[128,64]{0,1:T(8,128)S(1)} all-reduce(f32[128,64]{0,1:T(8,128)S(1)} %fusion.48), channel_id=1, replica_groups=mesh['section'=4,'expert'=4,'dp'=2] {'expert'}, use_global_device_ids=true, to_apply=%region_10.11 | all-reduce | flops 8192 | bytes 65536 | tf_op jit(solution)/shard_map/psum | solution.py:125
  113.8 9.4 %all-gather.2 = bf16[1,2048,64]{1,2,0:T(8,128)(2,1)S(1)} all-gather(bf16[1,512,64]{1,2,0:T(8,128)(2,1)S(1)} %copy-done.3), channel_id=4, replica_groups=mesh['section'=4,'expert'=4,'dp'=2] {'expert'}, dimensions={1}, use_global_device_ids=true | all-gather | bytes 327680 | tf_op jit(solution)/shard_map/all_gather | solution.py:123
  125.3 9.5 %fusion.20 = f32[160]{0:T(256)S(1)} fusion(bf16[1,3584,2048]{2,1,0:T(8,128)(2,1)} %param.19, bf16[160,2048]{1,0:T(8,128)(2,1)S(1)} %all_gather.23, f32[160,3584]{1,0:T(8,128)} %fusion.6, f32[160,3584]{1,0:T(8,128)} %fusion.2), kind=kOutput, calls=%fused_computation.23 | convolution fusion | flops 2353233664 | bytes 19923584 | tf_op jit(solution)/shard_map/dot_general | solution.py:66
  135.0 2.5 %all-reduce = f32[160]{0:T(256)S(1)} all-reduce(f32[160]{0:T(256)S(1)} %fusion.20), channel_id=6, replica_groups=mesh['section'=4,'expert'=4,'dp'=2] {'dp'}, use_global_device_ids=true, to_apply=%region_12.13.clone | all-reduce | flops 160 | bytes 1280
  140.3 1.3 fusion.47
  141.6 8.9 %all-reduce.1 = (f32[128,1]{0,1:T(1,128)S(1)}, f32[128,4]{0,1:T(4,128)S(1)}) all-reduce(f32[128,1]{0,1:T(1,128)S(1)} %bitcast.140, f32[128,4]{0,1:T(4,128)S(1)} %broadcast_multiply_fusion), channel_id=1, replica_groups=mesh['section'=4,'expert'=4,'dp'=2] {'expert'}, use_global_device_ids=true, to_apply=%region_17.18 | all-reduce | flops 640 | bytes 5120 | tf_op jit(solution)/shard_map/psum | solution.py:171
  151.6 3.4 %collective-permute-start = (bf16[128,512]{1,0:T(8,128)(2,1)S(1)}, bf16[128,512]{1,0:T(8,128)(2,1)S(1)}, u32[]{:S(2)}, u32[]{:S(2)}) collective-permute-start(bf16[128,512]{1,0:T(8,128)(2,1)S(1)} %fusion.28), channel_id=1, source_target_pairs={{8,0},{16,8},{24,16},{0,24},{9,1},{17,9},{25,17},{1,25},{10,2},{18... | collective-permute-start | bytes 393224 | tf_op jit(solution)/shard_map/ppermute | solution.py:18
  155.1 2.5 %collective-permute-done = bf16[128,512]{1,0:T(8,128)(2,1)S(1)} collective-permute-done((bf16[128,512]{1,0:T(8,128)(2,1)S(1)}, bf16[128,512]{1,0:T(8,128)(2,1)S(1)}, u32[]{:S(2)}, u32[]{:S(2)}) %collective-permute-start) | collective-permute-done | bytes 131104 | tf_op jit(solution)/shard_map/ppermute | solution.py:18
  158.2 1.6 copy.36
  159.8 1.6 copy.37
  (60 shorter events, 11.6 us)
Async XLA Ops:
  8.0 90.3 %copy-start = (bf16[1,64,512]{2,1,0:T(8,128)(2,1)S(1)}, bf16[1,64,512]{2,1,0:T(8,128)(2,1)}, u32[]{:S(2)}) copy-start(bf16[1,64,512]{2,1,0:T(8,128)(2,1)} %param.21) | copy-start | bytes 196612
  8.0 17.2 %copy-start.2 = (bf16[1,128,512]{2,1,0:T(8,128)(2,1)S(1)}, bf16[1,128,512]{2,1,0:T(8,128)(2,1)}, u32[]{:S(2)}) copy-start(bf16[1,128,512]{2,1,0:T(8,128)(2,1)} %param.12) | copy-start | bytes 393220
  8.0 132.3 %reduce-scatter.2.cloned.1.call-start = ((), (), s32[]{:S(2)}) async-start(), calls=%async_computation.1 | async-start | bytes 2359296 | tf_op jit(solution)/shard_map/reduce_scatter | solution.py:157
  40.0 10.2 %copy-start.1 = (bf16[1,2048,3584]{2,1,0:T(8,128)(2,1)S(1)}, bf16[1,2048,3584]{2,1,0:T(8,128)(2,1)}, u32[]{:S(2)}) copy-start(bf16[1,2048,3584]{2,1,0:T(8,128)(2,1)} %param.18) | copy-start | bytes 44040196
  96.4 1.7 %copy-start.6 = (s32[1,4]{1,0:T(1,128)S(1)}, s32[1,4]{1,0:T(1,128)}, u32[]{:S(2)}) copy-start(s32[1,4]{1,0:T(1,128)} %param.14) | copy-start | bytes 52
  96.4 17.4 %copy-start.3 = (bf16[1,512,64]{1,2,0:T(8,128)(2,1)S(1)}, bf16[1,512,64]{1,2,0:T(8,128)(2,1)}, u32[]{:S(2)}) copy-start(bf16[1,512,64]{1,2,0:T(8,128)(2,1)} %param.20) | copy-start | bytes 196612
  98.0 59.6 %all-reduce.5.cloned.1.call-start = ((), (), s32[]{:S(2)}) async-start(), calls=%async_computation.2 | async-start | bytes 524288 | tf_op jit(solution)/shard_map/psum | solution.py:136
  125.3 9.6 %copy-start.5 = (f32[1,2048]{1,0:T(1,128)S(1)}, f32[1,2048]{1,0:T(1,128)}, u32[]{:S(2)}) copy-start(f32[1,2048]{1,0:T(1,128)} %param.15) | copy-start | bytes 24580
  125.3 12.2 %copy-start.7 = (u32[32]{0:T(128)S(1)}, u32[32]{0:T(128)}, u32[]{:S(2)}) copy-start(u32[32]{0:T(128)} %constant.94) | copy-start | bytes 388
  134.9 15.7 %copy-start.4 = (bf16[1,2048,4]{1,2,0:T(4,128)(2,1)S(1)}, bf16[1,2048,4]{1,2,0:T(4,128)(2,1)}, u32[]{:S(2)}) copy-start(bf16[1,2048,4]{1,2,0:T(4,128)(2,1)} %param.16) | copy-start | bytes 49156
  151.6 6.0 %collective-permute-start = (bf16[128,512]{1,0:T(8,128)(2,1)S(1)}, bf16[128,512]{1,0:T(8,128)(2,1)S(1)}, u32[]{:S(2)}, u32[]{:S(2)}) collective-permute-start(bf16[128,512]{1,0:T(8,128)(2,1)S(1)} %fusion.28), channel_id=1, source_target_pairs={{8,0},{16,8},{24,16},{0,24},{9,1},{17,9},{25,17},{1,25},{10,2},{18... | collective-permute-start | bytes 393224 | tf_op jit(solution)/shard_map/ppermute | solution.py:18
Sparse Core Ops, SparseCore 0:
  98.1 42.1 reduce-scatter.1
Sparse Core Ops, SparseCore 1:
  125.4 18.3 all-reduce.4
where the time goes:
time: 169 us
  matrix products  66.8 us (40%)
  blocking collectives  66 us (39%)
  between operations  16.4 us (10%)
  local copies, waits for them, and re-layouts  9.96 us (6%)
  waiting for transfers between devices  3.87 us (2%)
  starting transfers between devices  3.51 us (2%)
  other arithmetic  2.28 us (1%)
    psum x1, blocking collectives, body(): lax.psum(jnp.dot(gradient_columns, backward_columns.T, preferred_element_...  15.4 us
    dot_general x1, matrix products, expert_back(): jnp.dot(d_up, expert_up_weight.T, preferred_element_type=jnp.float32)  12.7 us
    dot_general x1, matrix products, expert_back(): jnp.dot(d_gate, expert_gate_weight.T, preferred_element_type=jnp.float32)  12.1 us
    all_gather x1, blocking collectives, body(): lax.all_gather(s_cols, 'expert', axis=1, tiled=True)  12 us
    dot_general x1, matrix products, expert_back(): jnp.dot(adapter_gradient_list, expert_down_weight.T, preferred_element_ty...  11.6 us
    all_gather x1, blocking collectives, body(): lax.all_gather(gradient_columns, 'expert', axis=1, tiled=True)  9.67 us
    dot_general x1, matrix products, expert_back(): jnp.dot(hidden, expert_down_weight, preferred_element_type=jnp.float32)  9.53 us
    all_gather x1, blocking collectives, body(): a_full = lax.all_gather(down_map_rows, 'expert', axis=0, tiled=True)  9.38 us
  transfers between devices with their start and end apart: 3, of which 2 were waited for; matrix products, arithmetic and copies ran while one was open for 9% of the time, Pallas kernels for 0%

commit v1 on v0

--- a/solution.py
+++ b/solution.py
@@ -96,7 +96,7 @@
     gradient_columns = cotangent[0]
     count, width = s_cols.shape
     s_full, g_full = (
-        lax.all_gather(s_cols, "expert", axis=1, tiled=True),
+        jnp.concatenate(lax.all_gather(s_cols, "expert"), axis=1),
         lax.all_gather(gradient_columns, "expert", axis=1, tiled=True),
     )
     norm_gain_vector = layer_norm_gains[0]

time: 169 us -> 173 us (1.024)
  other arithmetic: 2.28 us -> 4.87 us
    unnamed x20 -> x49, local copies, waits for them, and re-layouts: 5.31 us -> 4.97 us
where the time goes in v1:
time: 173 us; the launch traced here: 172 us
  blocking collectives  67.1 us (39%)
  matrix products  66 us (38%)
  between operations  16.5 us (10%)
  local copies, waits for them, and re-layouts  10.4 us (6%)
  other arithmetic  4.87 us (3%)
  waiting for transfers between devices  3.95 us (2%)
  starting transfers between devices  3.48 us (2%)
    psum x1, blocking collectives, body(): lax.psum(jnp.dot(gradient_columns, backward_columns.T, preferred_element_...  15.4 us
    dot_general x1, matrix products, expert_back(): jnp.dot(d_up, expert_up_weight.T, preferred_element_type=jnp.float32)  12.8 us
    dot_general x1, matrix products, expert_back(): jnp.dot(d_gate, expert_gate_weight.T, preferred_element_type=jnp.float32)  12.1 us
    all_gather x1, blocking collectives, body(): lax.all_gather(s_cols, 'expert')  11.9 us
    dot_general x1, matrix products, expert_back(): jnp.dot(adapter_gradient_list, expert_down_weight.T, preferred_element_ty...  11.6 us
    all_gather x1, blocking collectives, body(): lax.all_gather(gradient_columns, 'expert', axis=1, tiled=True)  10.3 us
    dot_general x1, matrix products, expert_back(): jnp.dot(hidden, expert_down_weight, preferred_element_type=jnp.float32)  9.67 us
    all_gather x1, blocking collectives, body(): a_full = lax.all_gather(down_map_rows, 'expert', axis=0, tiled=True)  9.37 us
  transfers between devices with their start and end apart: 3, of which 2 were waited for; matrix products, arithmetic and copies ran while one was open for 9% of the time, Pallas kernels for 0%

profile of v1, /device:TPU:0, one launch (start us, length us, event | category | flops | bytes accessed | tf_op | source)
XLA Modules:
  0.0 172.3 jit_solution(14432971408479305235)
XLA Ops:
  8.1 11.9 %all_gather.21 = bf16[4,128,512]{2,1,0:T(8,128)(2,1)S(1)} all-gather(bf16[1,128,512]{2,1,0:T(8,128)(2,1)} %param.11), channel_id=1, replica_groups=mesh['section'=4,'expert'=4,'dp'=2] {'expert'}, dimensions={0}, use_global_device_ids=true | all-gather | bytes 655360 | tf_op jit(solution)/shard_map/all_gather | solution.py:99
  23.6 1.9 %all-gather.2 = f32[2,1,128]{2,1,0:T(1,128)S(1)} all-gather(f32[1,1,128]{2,1,0:T(1,128)S(1)} %bitcast.131), channel_id=1, replica_groups=mesh['section'=4,'expert'=4,'dp'=2] {'dp'}, dimensions={0}, use_global_device_ids=true | all-gather | bytes 1536 | tf_op jit(solution)/shard_map/all_gather | solution.py:149
  25.5 10.3 %all-gather = bf16[1,128,2048]{2,1,0:T(8,128)(2,1)} all-gather(bf16[1,128,512]{2,1,0:T(8,128)(2,1)S(1)} %copy-done.4), channel_id=2, replica_groups=mesh['section'=4,'expert'=4,'dp'=2] {'expert'}, dimensions={2}, use_global_device_ids=true | all-gather | bytes 655360 | tf_op jit(solution)/shard_map/all_gather | solution.py:100
  37.2 1.9 %all-gather.3 = f32[2,1,128]{2,1,0:T(1,128)S(1)} all-gather(f32[1,1,128]{2,1,0:T(1,128)S(1)} %bitcast.132), channel_id=1, replica_groups=mesh['section'=4,'expert'=4,'dp'=2] {'dp'}, dimensions={0}, use_global_device_ids=true | all-gather | bytes 1536 | tf_op jit(solution)/shard_map/all_gather | solution.py:150
  41.7 2.4 %all_gather.23 = bf16[160,2048]{1,0:T(8,128)(2,1)S(1)} all-gather(bf16[80,2048]{1,0:T(8,128)(2,1)S(1)} %convolution_convert_fusion.1), channel_id=1, replica_groups=mesh['section'=4,'expert'=4,'dp'=2] {'dp'}, dimensions={0}, use_global_device_ids=true | all-gather | bytes 983040 | tf_op jit(solution)/shard_map/all_gather | solution.py:145
  44.1 2.4 %all_gather.24 = bf16[160,2048]{1,0:T(8,128)(2,1)S(1)} all-gather(bf16[80,2048]{1,0:T(8,128)(2,1)S(1)} %convolution_convert_fusion), channel_id=1, replica_groups=mesh['section'=4,'expert'=4,'dp'=2] {'dp'}, dimensions={0}, use_global_device_ids=true | all-gather | bytes 983040 | tf_op jit(solution)/shard_map/all_gather | solution.py:144
  46.6 9.3 %fusion.2 = f32[160,3584]{1,0:T(8,128)} fusion(bf16[160,2048]{1,0:T(8,128)(2,1)S(1)} %all_gather.24, bf16[1,2048,3584]{2,1,0:T(8,128)(2,1)} %param.17), kind=kOutput, calls=%fused_computation.2 | convolution fusion | flops 2348810240 | bytes 17629184 | tf_op jit(solution)/shard_map/dot_general | solution.py:61
  55.9 3.9 %fusion.6 = f32[160,3584]{1,0:T(8,128)} fusion(bf16[160,2048]{1,0:T(8,128)(2,1)S(1)} %all_gather.24, bf16[1,2048,3584]{2,1,0:T(8,128)(2,1)S(1)} %bitcast.116), kind=kOutput, calls=%fused_computation.6 | convolution fusion | flops 2348810240 | bytes 17629184 | tf_op jit(solution)/shard_map/dot_general | solution.py:62
  59.8 11.6 %fusion.10 = f32[160,3584]{1,0:T(8,128)} fusion(bf16[160,2048]{1,0:T(8,128)(2,1)S(1)} %all_gather.23, bf16[1,3584,2048]{2,1,0:T(8,128)(2,1)} %param.19), kind=kOutput, calls=%fused_computation.10 | convolution fusion | flops 2348810240 | bytes 17629184 | tf_op jit(solution)/shard_map/dot_general | solution.py:68
  71.4 12.1 %fusion = f32[160,2048]{1,0:T(8,128)S(1)} fusion(bf16[1,2048,3584]{2,1,0:T(8,128)(2,1)} %param.17, f32[160,3584]{1,0:T(8,128)} %fusion.2, f32[160,3584]{1,0:T(8,128)} %fusion.10, f32[160,3584]{1,0:T(8,128)} %fusion.6), kind=kOutput, calls=%fused_computation | convolution fusion | flops 2354544640 | bytes 22872064 | tf_op jit(solution)/shard_map/dot_general | solution.py:71
  83.5 12.8 %fusion.15 = f32[160,2048]{1,0:T(8,128)} fusion(f32[160,2048]{1,0:T(8,128)S(1)} %fusion, bf16[1,2048,3584]{2,1,0:T(8,128)(2,1)} %param.18, f32[160,3584]{1,0:T(8,128)} %fusion.10, f32[160,3584]{1,0:T(8,128)} %fusion.2), kind=kOutput, calls=%fused_computation.13 | convolution fusion | flops 2352578560 | bytes 21889024 | tf_op jit(solution)/shard_map/dot_general | solution.py:71
  96.3 2.2 %reshape.180 = f32[2,80,4,512]{3,2,1,0:T(4,128)S(1)} reshape(f32[160,2048]{1,0:T(8,128)} %fusion.15) | data formatting | bytes 2621440 | tf_op jit(solution)/shard_map/reshape | solution.py:154
  98.5 1.5 multiply_bitcast_fusion
  100.0 1.6 copy.35
  102.1 15.4 %psum.35 = f32[128,64]{0,1:T(8,128)S(1)} all-reduce(f32[128,64]{0,1:T(8,128)S(1)} %fusion.38), channel_id=1, replica_groups=mesh['section'=4,'expert'=4,'dp'=2] {'expert'}, use_global_device_ids=true, to_apply=%region_10.11 | all-reduce | flops 8192 | bytes 65536 | tf_op jit(solution)/shard_map/psum | solution.py:125
  117.5 9.4 %all-gather.1 = bf16[1,2048,64]{1,2,0:T(8,128)(2,1)S(1)} all-gather(bf16[1,512,64]{1,2,0:T(8,128)(2,1)S(1)} %copy-done.5), channel_id=3, replica_groups=mesh['section'=4,'expert'=4,'dp'=2] {'expert'}, dimensions={1}, use_global_device_ids=true | all-gather | bytes 327680 | tf_op jit(solution)/shard_map/all_gather | solution.py:123
  129.0 9.7 %fusion.20 = f32[160]{0:T(256)S(1)} fusion(bf16[1,3584,2048]{2,1,0:T(8,128)(2,1)} %param.19, bf16[160,2048]{1,0:T(8,128)(2,1)S(1)} %all_gather.23, f32[160,3584]{1,0:T(8,128)} %fusion.6, f32[160,3584]{1,0:T(8,128)} %fusion.2), kind=kOutput, calls=%fused_computation.23 | convolution fusion | flops 2353233664 | bytes 19923584 | tf_op jit(solution)/shard_map/dot_general | solution.py:66
  138.7 2.5 %all-reduce = f32[160]{0:T(256)S(1)} all-reduce(f32[160]{0:T(256)S(1)} %fusion.20), channel_id=5, replica_groups=mesh['section'=4,'expert'=4,'dp'=2] {'dp'}, use_global_device_ids=true, to_apply=%region_12.13.clone | all-reduce | flops 160 | bytes 1280
  142.6 1.4 reduce-scatter.2.cloned.1.call-done
  145.3 8.9 %all-reduce.1 = (f32[128,1]{0,1:T(1,128)S(1)}, f32[128,4]{0,1:T(4,128)S(1)}) all-reduce(f32[128,1]{0,1:T(1,128)S(1)} %bitcast.128, f32[128,4]{0,1:T(4,128)S(1)} %broadcast_multiply_fusion), channel_id=1, replica_groups=mesh['section'=4,'expert'=4,'dp'=2] {'expert'}, use_global_device_ids=true, to_apply=%region_17.18 | all-reduce | flops 640 | bytes 5120 | tf_op jit(solution)/shard_map/psum | solution.py:171
  155.1 3.4 %collective-permute-start = (bf16[128,512]{1,0:T(8,128)(2,1)S(1)}, bf16[128,512]{1,0:T(8,128)(2,1)S(1)}, u32[]{:S(2)}, u32[]{:S(2)}) collective-permute-start(bf16[128,512]{1,0:T(8,128)(2,1)S(1)} %fusion.28), channel_id=1, source_target_pairs={{8,0},{16,8},{24,16},{0,24},{9,1},{17,9},{25,17},{1,25},{10,2},{18... | collective-permute-start | bytes 393224 | tf_op jit(solution)/shard_map/ppermute | solution.py:18
  158.5 2.5 %collective-permute-done = bf16[128,512]{1,0:T(8,128)(2,1)S(1)} collective-permute-done((bf16[128,512]{1,0:T(8,128)(2,1)S(1)}, bf16[128,512]{1,0:T(8,128)(2,1)S(1)}, u32[]{:S(2)}, u32[]{:S(2)}) %collective-permute-start) | collective-permute-done | bytes 131104 | tf_op jit(solution)/shard_map/ppermute | solution.py:18
  161.7 1.6 copy.44
  163.3 1.6 copy.45
  (95 shorter events, 13.7 us)
Async XLA Ops:
  8.0 93.9 %copy-start = (bf16[1,64,512]{2,1,0:T(8,128)(2,1)S(1)}, bf16[1,64,512]{2,1,0:T(8,128)(2,1)}, u32[]{:S(2)}) copy-start(bf16[1,64,512]{2,1,0:T(8,128)(2,1)} %param.21) | copy-start | bytes 196612
  8.0 12.6 %copy-start.15 = (s32[1,128,2]{1,2,0:T(2,128)S(1)}, s32[1,128,2]{1,2,0:T(2,128)}, u32[]{:S(2)}) copy-start(s32[1,128,2]{1,2,0:T(2,128)} %param.13) | copy-start | bytes 3076
  8.0 13.2 %copy-start.8 = (f32[1,2048]{1,0:T(1,128)S(1)}, f32[1,2048]{1,0:T(1,128)}, u32[]{:S(2)}) copy-start(f32[1,2048]{1,0:T(1,128)} %param.15) | copy-start | bytes 24580
  8.0 135.9 %reduce-scatter.2.cloned.1.call-start = ((), (), s32[]{:S(2)}) async-start(), calls=%async_computation.1 | async-start | bytes 2359296 | tf_op jit(solution)/shard_map/reduce_scatter | solution.py:157
  20.2 3.0 %copy-start.7 = (bf16[1,2048,4]{1,2,0:T(4,128)(2,1)S(1)}, bf16[1,2048,4]{1,2,0:T(4,128)(2,1)}, u32[]{:S(2)}) copy-start(bf16[1,2048,4]{1,2,0:T(4,128)(2,1)} %param.16) | copy-start | bytes 49156
  20.2 5.3 %copy-start.4 = (bf16[1,128,512]{2,1,0:T(8,128)(2,1)S(1)}, bf16[1,128,512]{2,1,0:T(8,128)(2,1)}, u32[]{:S(2)}) copy-start(bf16[1,128,512]{2,1,0:T(8,128)(2,1)} %param.12) | copy-start | bytes 393220
  20.6 4.9 %copy-start.9 = (f32[4]{0:T(128)}, f32[4]{0:T(128)S(1)}, u32[]{:S(2)}) copy-start(f32[4]{0:T(128)S(1)} %compare_convert_fusion) | copy-start | bytes 52
  23.2 32.6 %slice-start = ((s8[14680064]{0:T(1024)(128)(4,1)}), s8[2097152]{0:T(1024)(128)(4,1)S(1)}, s32[]{:S(2)}) async-start(s8[14680064]{0:T(1024)(128)(4,1)} %bitcast.115), calls=%async_computation.3 | async-start | bytes 4194304
  23.6 17.9 %copy-start.11 = (pred[128]{0:T(512)(128)(4,1)}, pred[128]{0:T(512)(128)(4,1)S(1)}, u32[]{:S(2)}) copy-start(pred[128]{0:T(512)(128)(4,1)S(1)} %convert_compare_fusion) | copy-start | bytes 388
  37.1 4.3 %copy-start.3 = (bf16[1,128,2048]{2,1,0:T(8,128)(2,1)S(1)}, bf16[1,128,2048]{2,1,0:T(8,128)(2,1)}, u32[]{:S(2)}) copy-start(bf16[1,128,2048]{2,1,0:T(8,128)(2,1)} %all-gather) | copy-start | bytes 1572868
  39.8 6.8 %copy-start.13 = (s32[128]{0:T(128)}, s32[128]{0:T(128)S(1)}, u32[]{:S(2)}) copy-start(s32[128]{0:T(128)S(1)} %convert_subtract_fusion.1) | copy-start | bytes 1540
  41.7 14.2 %slice-start.1 = ((s8[14680064]{0:T(1024)(128)(4,1)}), s8[4194304]{0:T(1024)(128)(4,1)S(1)}, s32[]{:S(2)}) async-start(s8[14680064]{0:T(1024)(128)(4,1)} %bitcast.115), calls=%async_computation.4 | async-start | bytes 8388608
  46.6 9.3 %slice-start.2 = ((s8[14680064]{0:T(1024)(128)(4,1)}), s8[4194304]{0:T(1024)(128)(4,1)S(1)}, s32[]{:S(2)}) async-start(s8[14680064]{0:T(1024)(128)(4,1)} %bitcast.115), calls=%async_computation.5 | async-start | bytes 8388608
  46.6 9.3 %slice-start.3 = ((s8[14680064]{0:T(1024)(128)(4,1)}), s8[4194304]{0:T(1024)(128)(4,1)S(1)}, s32[]{:S(2)}) async-start(s8[14680064]{0:T(1024)(128)(4,1)} %bitcast.115), calls=%async_computation.6 | async-start | bytes 8388608
  100.0 17.4 %copy-start.5 = (bf16[1,512,64]{1,2,0:T(8,128)(2,1)S(1)}, bf16[1,512,64]{1,2,0:T(8,128)(2,1)}, u32[]{:S(2)}) copy-start(bf16[1,512,64]{1,2,0:T(8,128)(2,1)} %param.20) | copy-start | bytes 196612
  101.7 59.4 %all-reduce.5.cloned.1.call-start = ((), (), s32[]{:S(2)}) async-start(), calls=%async_computation.2 | async-start | bytes 524288 | tf_op jit(solution)/shard_map/psum | solution.py:136
  129.0 12.2 %copy-start.17 = (u32[32]{0:T(128)S(1)}, u32[32]{0:T(128)}, u32[]{:S(2)}) copy-start(u32[32]{0:T(128)} %constant.93) | copy-start | bytes 388
  129.0 13.3 %copy-start.12 = (pred[128]{0:T(512)(128)(4,1)S(1)}, pred[128]{0:T(512)(128)(4,1)}, u32[]{:S(2)}) copy-start(pred[128]{0:T(512)(128)(4,1)} %copy-done.11) | copy-start | bytes 388
  129.0 13.3 %copy-start.14 = (s32[128]{0:T(128)S(1)}, s32[128]{0:T(128)}, u32[]{:S(2)}) copy-start(s32[128]{0:T(128)} %copy-done.13) | copy-start | bytes 1540
  129.0 13.5 %copy-start.10 = (f32[4]{0:T(128)S(1)}, f32[4]{0:T(128)}, u32[]{:S(2)}) copy-start(f32[4]{0:T(128)} %copy-done.9) | copy-start | bytes 52
  129.0 15.0 %copy-start.1 = (f32[128,2048]{1,0:T(8,128)S(1)}, f32[128,2048]{1,0:T(8,128)}, u32[]{:S(2)}) copy-start(f32[128,2048]{1,0:T(8,128)} %copy.37) | copy-start | bytes 3145732
  129.0 15.0 %copy-start.6 = (bf16[1,512,64]{1,2,0:T(8,128)(2,1)S(1)}, bf16[1,512,64]{1,2,0:T(8,128)(2,1)}, u32[]{:S(2)}) copy-start(bf16[1,512,64]{1,2,0:T(8,128)(2,1)} %param.20) | copy-start | bytes 196612
  129.0 25.2 %copy-start.2 = (f32[4,128,512]{1,2,0:T(8,128)S(1)}, f32[4,128,512]{1,2,0:T(8,128)}, u32[]{:S(2)}) copy-start(f32[4,128,512]{1,2,0:T(8,128)} %get-tuple-element.15) | copy-start | bytes 3145732
  155.1 5.9 %collective-permute-start = (bf16[128,512]{1,0:T(8,128)(2,1)S(1)}, bf16[128,512]{1,0:T(8,128)(2,1)S(1)}, u32[]{:S(2)}, u32[]{:S(2)}) collective-permute-start(bf16[128,512]{1,0:T(8,128)(2,1)S(1)} %fusion.28), channel_id=1, source_target_pairs={{8,0},{16,8},{24,16},{0,24},{9,1},{17,9},{25,17},{1,25},{10,2},{18... | collective-permute-start | bytes 393224 | tf_op jit(solution)/shard_map/ppermute | solution.py:18
  (1 other events, 1.7 us)
Sparse Core Ops, SparseCore 0:
  101.8 42.1 reduce-scatter.1
Sparse Core Ops, SparseCore 1:
  129.0 18.3 all-reduce.4
